TPU v7x, 256 devices: a 2x2x32 block of a 4x8x32 slice. The times are simulated.
256 devices in a mesh: group: 4 (over y, x), col: 64 (over z, core).
Axes of the slice: x: 2, y: 2, z: 32, core: 2. Of those that a mesh axis runs over, the one named last changes fastest.
The devices are a block of a 4x8x32 slice.
Arguments:
- homolog_embedding: bfloat16 [384, 256, 256], P('group', 'col'), parts along dimension 0, may hold values from -6 to 6
- left_factor_matrix: bfloat16 [256, 32], replicated, may hold values from -0.375 to 0.375
- right_factor_matrix: bfloat16 [256, 32], replicated, may hold values from -0.375 to 0.375
- decoder: bfloat16 [1024, 128], replicated, may hold values from -2 to 2
- pair_output_bias: float32 [128], replicated, may hold values from -3 to 3
- pair_output_gradient: bfloat16 [1024, 256, 128], P('group', 'col'), parts along dimension 0, may hold values from -16 to 16
Outputs:
- first_operand_gradient: float32 [384, 256, 32], P('group', 'col'), parts along dimension 0
- second_operand_gradient: float32 [384, 256, 32], P('group', 'col'), parts along dimension 0
- alignment_gradient: bfloat16 [384, 256, 256], P('group', 'col'), parts along dimension 0
There are 4 independent parts, one for each index of `group`. A program takes and returns all parts, laid end to end along the dimension named above; an argument that names none is the same for every part. Nothing has to cross between parts.
All inputs are finite; a program needn't handle non-finite values.
Results may differ from a plain program's by a relative error of at most 0.0083.
Values may be sent and summed in bfloat16 or wider, within the bound.
No kernel may reach another device: no remote copies, remote signals or barrier semaphores. Data moves between devices by JAX's collectives and lax.ppermute only.
A program may use at most 64 MiB of HBM per device.

v0:
```python
import jax
import jax.numpy as jnp
from jax import lax
from jax.sharding import PartitionSpec as P


def in_one_piece(arrays, axis, dim, along):
    widths = [a.shape[along] for a in arrays]
    both = jnp.concatenate(arrays, axis=along)
    whole = lax.all_gather(both, axis, axis=dim, tiled=True)
    return tuple(jnp.split(whole, [sum(widths[:k]) for k in range(1, len(widths))], axis=along))


def per_device(
    homolog_embedding,
    left_factor_matrix,
    right_factor_matrix,
    decoder,
    pair_output_bias,
    pair_output_gradient,
):
    alignment_row_count, local_residue_start, alignment_channel_width = homolog_embedding.shape
    operand_channel_width = left_factor_matrix.shape[1]
    channels = decoder.shape[1]
    residue_total_count = local_residue_start * lax.axis_size("col")
    reciprocal_rows = 1.0 / alignment_row_count
    block_res = local_residue_start * max(1, 96 // local_residue_start)
    alignment_flattened_rows = homolog_embedding.reshape(
        alignment_row_count * local_residue_start, alignment_channel_width
    )
    first_operand_rows = (
        jnp.dot(alignment_flattened_rows, left_factor_matrix, preferred_element_type=jnp.float32)
        .astype(jnp.bfloat16)
        .reshape(alignment_row_count, local_residue_start * operand_channel_width)
    )
    second_operand_rows = (
        jnp.dot(alignment_flattened_rows, right_factor_matrix, preferred_element_type=jnp.float32)
        .astype(jnp.bfloat16)
        .reshape(alignment_row_count, local_residue_start * operand_channel_width)
    )
    second_operand_local = second_operand_rows.reshape(
        alignment_row_count, local_residue_start, operand_channel_width
    )

    def outer_slopes(slope_rows, rows_by_length, col_span):
        backward = (
            jnp.dot(slope_rows, decoder.T, preferred_element_type=jnp.float32) * reciprocal_rows
        )
        return backward.astype(jnp.bfloat16).reshape(
            rows_by_length, col_span, operand_channel_width, operand_channel_width
        )

    offset_col = jnp.int32(0)
    second_operand_gradient = jnp.zeros(
        (alignment_row_count, local_residue_start, operand_channel_width), jnp.float32
    )
    stored = jnp.zeros((residue_total_count, local_residue_start * channels), jnp.bfloat16)
    left_segment, right_segment = in_one_piece(
        (first_operand_rows, second_operand_rows), "col", 1, 0
    )
    right_whole = right_segment
    piece_res = left_segment.shape[1] // operand_channel_width
    first_res = offset_col // operand_channel_width
    collected = []
    for split_offset in range(0, piece_res, block_res):
        split_rows_by_length = min(block_res, piece_res - split_offset)
        split_left_block = left_segment[
            :,
            split_offset
            * operand_channel_width : (split_offset + split_rows_by_length)
            * operand_channel_width,
        ].reshape(alignment_row_count, split_rows_by_length, operand_channel_width)
        collected.append((split_rows_by_length, split_left_block, first_res + split_offset))
    for rows_by_length, left_block, first_row in collected:
        products = (
            jnp.einsum(
                "sic,sjd->ijcd",
                left_block,
                second_operand_local,
                preferred_element_type=jnp.float32,
            )
            * reciprocal_rows
        )
        products = products.astype(jnp.bfloat16).reshape(
            rows_by_length * local_residue_start, operand_channel_width * operand_channel_width
        )
        linear = jnp.dot(products, decoder, preferred_element_type=jnp.float32) + pair_output_bias
        upstream = lax.dynamic_slice_in_dim(pair_output_gradient, first_row, rows_by_length, 0)
        upstream = upstream.reshape(rows_by_length * local_residue_start, channels).astype(
            jnp.float32
        )
        accumulate_slope_rows = (upstream * 2.0 * jnp.maximum(linear, 0.0)).astype(jnp.bfloat16)
        stored = lax.dynamic_update_slice_in_dim(
            stored,
            accumulate_slope_rows.reshape(rows_by_length, local_residue_start * channels),
            first_row,
            0,
        )
        accumulate_slopes = outer_slopes(accumulate_slope_rows, rows_by_length, local_residue_start)
        second_operand_gradient = second_operand_gradient + jnp.einsum(
            "ijcd,sic->sjd", accumulate_slopes, left_block, preferred_element_type=jnp.float32
        )
    second_operand_gradient, stored, right_whole = (second_operand_gradient, stored, right_whole)
    received = lax.all_to_all(stored, "col", split_axis=0, concat_axis=1, tiled=True)
    right_all = right_whole.reshape(alignment_row_count, residue_total_count, operand_channel_width)
    col_span = local_residue_start * max(
        max(1, 96 // local_residue_start), lax.axis_size("col") // 8
    )
    first_operand_gradient = jnp.zeros(
        (alignment_row_count, local_residue_start, operand_channel_width), jnp.float32
    )
    for offset in range(0, residue_total_count, col_span):
        width_cols = min(col_span, residue_total_count - offset)
        slope_rows = received[:, offset * channels : (offset + width_cols) * channels].reshape(
            local_residue_start * width_cols, channels
        )
        slopes = outer_slopes(slope_rows, local_residue_start, width_cols)
        first_operand_gradient = first_operand_gradient + jnp.einsum(
            "ijcd,sjd->sic",
            slopes,
            right_all[:, offset : offset + width_cols],
            preferred_element_type=jnp.float32,
        )
    first_operand_gradient_step = first_operand_gradient.astype(jnp.bfloat16).reshape(
        alignment_row_count * local_residue_start, operand_channel_width
    )
    second_operand_gradient_step = second_operand_gradient.astype(jnp.bfloat16).reshape(
        alignment_row_count * local_residue_start, operand_channel_width
    )
    alignment_gradient = jnp.dot(
        first_operand_gradient_step, left_factor_matrix.T, preferred_element_type=jnp.float32
    ) + jnp.dot(
        second_operand_gradient_step, right_factor_matrix.T, preferred_element_type=jnp.float32
    )
    alignment_gradient = alignment_gradient.astype(jnp.bfloat16).reshape(
        alignment_row_count, local_residue_start, alignment_channel_width
    )
    return (first_operand_gradient, second_operand_gradient, alignment_gradient)


def solution(mesh):
    placed = (P("group", "col", None), P(), P(), P(), P(), P("group", "col", None))
    return jax.shard_map(
        per_device,
        mesh=mesh,
        in_specs=placed,
        out_specs=(P("group", "col", None), P("group", "col", None), P("group", "col", None)),
        check_vma=False,
    )
```

profile of v0, /device:TPU:38, one launch (start us, length us, event | category | flops | bytes accessed | tf_op | source)
XLA Modules:
  0.0 278.4 jit_solution(2728740958674817468)
XLA Ops:
  11.3 1.6 convert_multiply_fusion.2
  12.9 1.8 convert_multiply_fusion
  14.7 143.4 %all-gather.2.cloned.1.call-done = bf16[192,8192]{1,0:T(8,128)(2,1)} async-done(((bf16[192,128]{1,0:T(8,128)(2,1)}), bf16[192,8192]{1,0:T(8,128)(2,1)}) %all-gather.2.cloned.1.call-update) | async-done | bytes 3145744 | tf_op jit(solution)/shard_map/all_gather | solution.py:10
  158.1 2.1 fusion.42
  163.8 5.4 %copy.31 = bf16[96,4,32,32]{3,2,1,0:T(8,128)(2,1)S(1)} copy(bf16[96,4,32,32]{0,3,2,1:T(8,128)(2,1)} %fusion.5) | data formatting | bytes 1572864 | tf_op jit(solution)/shard_map/convert_element_type | solution.py:84
  169.2 4.0 %reshape.105 = bf16[384,1024]{1,0:T(8,128)(2,1)} reshape(bf16[96,4,32,32]{3,2,1,0:T(8,128)(2,1)S(1)} %copy.31) | data formatting | bytes 1572864 | tf_op jit(solution)/shard_map/reshape | solution.py:84
  180.2 5.4 %copy.27 = bf16[96,4,32,32]{3,2,1,0:T(8,128)(2,1)S(1)} copy(bf16[96,4,32,32]{0,3,2,1:T(8,128)(2,1)} %fusion.4) | data formatting | bytes 1572864 | tf_op jit(solution)/shard_map/convert_element_type | solution.py:84
  185.6 4.0 %reshape.102 = bf16[384,1024]{1,0:T(8,128)(2,1)} reshape(bf16[96,4,32,32]{3,2,1,0:T(8,128)(2,1)S(1)} %copy.27) | data formatting | bytes 1572864 | tf_op jit(solution)/shard_map/reshape | solution.py:84
  194.6 3.2 %copy.35 = bf16[64,4,32,32]{3,2,1,0:T(8,128)(2,1)S(1)} copy(bf16[64,4,32,32]{0,3,2,1:T(8,128)(2,1)S(1)} %fusion.6) | data formatting | bytes 1048576 | tf_op jit(solution)/shard_map/convert_element_type | solution.py:84
  197.9 2.2 reshape.108
  201.4 14.5 %all-to-all-start = ((bf16[64,4,512]{2,1,0:T(4,128)(2,1)}), bf16[64,4,512]{2,1,0:T(4,128)(2,1)}, u32[]{:S(2)}, u32[]{:S(2)}) async-start(bf16[64,4,512]{2,1,0:T(4,128)(2,1)} %all_to_all.14), calls=%async_computation | async-start | bytes 524288 | tf_op jit(solution)/shard_map/all_to_all | solution.py:104
  216.0 2.7 split.5
  218.6 3.1 %copy.21 = bf16[96,8192]{0,1:T(8,128)(2,1)S(1)} copy(bf16[96,8192]{1,0:T(8,128)(2,1)} %split.5) | data formatting | bytes 3145728 | tf_op jit(solution)/shard_map/split | solution.py:11
  223.8 2.8 %copy.72 = bf16[96,96,32]{1,0,2:T(8,128)(2,1)} copy(bf16[96,96,32]{0,2,1:T(8,128)(2,1)} %get-tuple-element.6) | data formatting | bytes 1179648
  226.6 1.8 copy.71
  229.7 3.8 %reshape.116 = bf16[96,4,32,32]{3,2,1,0:T(8,128)(2,1)S(1)} reshape(bf16[384,1024]{1,0:T(8,128)(2,1)} %multiply_convert_fusion.4) | data formatting | bytes 1572864 | tf_op jit(solution)/shard_map/reshape | solution.py:49
  234.7 4.9 %reshape.117 = bf16[96,4,32,32]{3,2,1,0:T(8,128)(2,1)} reshape(bf16[384,1024]{1,0:T(8,128)(2,1)} %multiply_convert_fusion.3) | data formatting | bytes 1572864 | tf_op jit(solution)/shard_map/reshape | solution.py:49
  240.7 3.7 %reshape.118 = bf16[64,4,32,32]{3,2,1,0:T(8,128)(2,1)} reshape(bf16[256,1024]{1,0:T(8,128)(2,1)} %fusion.8) | data formatting | bytes 1048576 | tf_op jit(solution)/shard_map/reshape | solution.py:49
  244.5 4.7 %fusion.20 = f32[96,4,32]{0,2,1:T(8,128)S(1)} fusion(bf16[96,4,32,32]{3,2,1,0:T(8,128)(2,1)S(1)} %reshape.116, bf16[96,96,32]{1,0,2:T(8,128)(2,1)} %copy-done.5), kind=kOutput, calls=%fused_computation.34 | convolution fusion | flops 75497472 | bytes 1425408 | tf_op jit(solution)/shard_map/ijcd,sic->sjd/dot_general | solution.py:100
  249.2 3.5 %fusion.27 = f32[96,4,32]{0,2,1:T(8,128)S(1)} fusion(f32[96,4,32]{0,2,1:T(8,128)S(1)} %fusion.20, bf16[96,4,32,32]{3,2,1,0:T(8,128)(2,1)S(1)} %copy-done.1, bf16[96,96,32]{1,0,2:T(8,128)(2,1)S(1)} %copy-done.4), kind=kOutput, calls=%fused_computation.40 | convolution fusion | flops 75509760 | bytes 1474560 | tf_op jit(solution)/shard_map/ijcd,sic->sjd/dot_general | solution.py:100
  254.2 3.3 %all-to-all-done = bf16[64,4,512]{2,1,0:T(4,128)(2,1)} async-done(((bf16[64,4,512]{2,1,0:T(4,128)(2,1)}), bf16[64,4,512]{2,1,0:T(4,128)(2,1)}, u32[]{:S(2)}, u32[]{:S(2)}) %all-to-all-start) | async-done | bytes 262176 | tf_op jit(solution)/shard_map/all_to_all | solution.py:104
  261.8 1.6 reshape.111
  265.4 2.1 convolution_bitcast_fusion.1
  268.4 2.0 fusion.45
  (99 shorter events, 36.1 us)
Async XLA Ops:
  7.2 166.1 %copy-start = (bf16[1024,128]{1,0:T(8,128)(2,1)S(1)}, bf16[1024,128]{1,0:T(8,128)(2,1)}, u32[]{:S(2)}) copy-start(bf16[1024,128]{1,0:T(8,128)(2,1)} %param.9) | copy-start | bytes 786436
  7.2 150.9 %all-gather.2.cloned.1.call-start = ((), (), s32[]{:S(2)}) async-start(), calls=%async_computation.1 | async-start | bytes 3194880 | tf_op jit(solution)/shard_map/all_gather | solution.py:10
  161.5 0.9 copy-start.3
  169.2 4.0 %copy-start.21 = (f32[128]{0:T(128)S(1)}, f32[128]{0:T(128)}, u32[]{:S(2)}) copy-start(f32[128]{0:T(128)} %param.10) | copy-start | bytes 1540
  177.9 0.9 copy-start.5
  191.1 0.7 copy-start.10
  193.2 0.8 copy-start.6
  197.9 2.3 copy-start.15
  197.9 2.6 copy-start.18
  197.9 2.7 copy-start.17
  200.5 18.2 %copy-start.13 = (bf16[256,128]{1,0:T(8,128)(2,1)}, bf16[256,128]{1,0:T(8,128)(2,1)S(1)}, u32[]{:S(2)}) copy-start(bf16[256,128]{1,0:T(8,128)(2,1)S(1)} %fusion.18) | copy-start | bytes 196612
  201.4 56.2 %all-to-all-start = ((bf16[64,4,512]{2,1,0:T(4,128)(2,1)}), bf16[64,4,512]{2,1,0:T(4,128)(2,1)}, u32[]{:S(2)}, u32[]{:S(2)}) async-start(bf16[64,4,512]{2,1,0:T(4,128)(2,1)} %all_to_all.14), calls=%async_computation | async-start | bytes 524288 | tf_op jit(solution)/shard_map/all_to_all | solution.py:104
  223.8 4.6 %copy-start.11 = (bf16[384,128]{1,0:T(8,128)(2,1)S(1)}, bf16[384,128]{1,0:T(8,128)(2,1)}, u32[]{:S(2)}) copy-start(bf16[384,128]{1,0:T(8,128)(2,1)} %copy-done.10) | copy-start | bytes 294916
  234.7 4.9 %copy-start.14 = (bf16[256,128]{1,0:T(8,128)(2,1)S(1)}, bf16[256,128]{1,0:T(8,128)(2,1)}, u32[]{:S(2)}) copy-start(bf16[256,128]{1,0:T(8,128)(2,1)} %copy-done.13) | copy-start | bytes 196612
  244.5 4.7 %copy-start.1 = (bf16[96,4,32,32]{3,2,1,0:T(8,128)(2,1)S(1)}, bf16[96,4,32,32]{3,2,1,0:T(8,128)(2,1)}, u32[]{:S(2)}) copy-start(bf16[96,4,32,32]{3,2,1,0:T(8,128)(2,1)} %reshape.117) | copy-start | bytes 2359300
  244.5 4.7 %copy-start.4 = (bf16[96,96,32]{1,0,2:T(8,128)(2,1)S(1)}, bf16[96,96,32]{1,0,2:T(8,128)(2,1)}, u32[]{:S(2)}) copy-start(bf16[96,96,32]{1,0,2:T(8,128)(2,1)} %copy-done.3) | copy-start | bytes 1769476
  249.2 3.6 %copy-start.2 = (bf16[64,4,32,32]{3,2,1,0:T(8,128)(2,1)S(1)}, bf16[64,4,32,32]{3,2,1,0:T(8,128)(2,1)}, u32[]{:S(2)}) copy-start(bf16[64,4,32,32]{3,2,1,0:T(8,128)(2,1)} %reshape.118) | copy-start | bytes 1572868
  249.2 3.6 %copy-start.7 = (bf16[96,2048]{0,1:T(8,128)(2,1)S(1)}, bf16[96,2048]{0,1:T(8,128)(2,1)}, u32[]{:S(2)}) copy-start(bf16[96,2048]{0,1:T(8,128)(2,1)} %copy-done.6) | copy-start | bytes 1179652
  264.0 3.5 %copy-start.8 = (bf16[4,96,32,32]{1,0,3,2:T(4,128)(2,1)S(1)}, bf16[4,96,32,32]{1,0,3,2:T(4,128)(2,1)}, u32[]{:S(2)}) copy-start(bf16[4,96,32,32]{1,0,3,2:T(4,128)(2,1)} %reshape.111) | copy-start | bytes 2359300
  265.4 2.1 copy-start.12
  265.4 2.9 %copy-start.9 = (bf16[4,64,32,32]{1,0,3,2:T(4,128)(2,1)S(1)}, bf16[4,64,32,32]{1,0,3,2:T(4,128)(2,1)}, u32[]{:S(2)}) copy-start(bf16[4,64,32,32]{1,0,3,2:T(4,128)(2,1)} %reshape.115) | copy-start | bytes 1572868
  265.4 2.9 %copy-start.16 = (bf16[96,64,32]{0,2,1:T(8,128)(2,1)S(1)}, bf16[96,64,32]{0,2,1:T(8,128)(2,1)}, u32[]{:S(2)}) copy-start(bf16[96,64,32]{0,2,1:T(8,128)(2,1)} %slice.49) | copy-start | bytes 1179652
  268.3 2.1 copy-start.19
  268.3 2.3 copy-start.20
Sparse Core Ops, SparseCore 0:
  11.4 146.6 all-gather.1
where the time goes:
time: 279 us; the launch traced here: 278 us
  waiting for transfers between devices  147 us (53%)
  local copies, waits for them, and re-layouts  70.5 us (25%)
  matrix products  28 us (10%)
  starting transfers between devices  14.6 us (5%)
  between operations  14.6 us (5%)
  other arithmetic  3.96 us (1%)
    all_gather x1, waiting for transfers between devices, in_one_piece(): whole = lax.all_gather(both, axis, axis=dim, tiled=True)  143 us
    reshape x6, local copies, waits for them, and re-layouts, outer_slopes(): backward.astype(jnp.bfloat16)  16 us
    all_to_all x1, starting transfers between devices, per_device(): lax.all_to_all(stored, 'col', split_axis=0, concat_axis=1, tiled=True)  14.5 us
    convert_element_type x3, local copies, waits for them, and re-layouts, per_device(): products.astype(jnp.bfloat16)  14 us
    reshape x3, local copies, waits for them, and re-layouts, per_device(): products.astype(jnp.bfloat16)  10.3 us
    dot_general x3, matrix products, per_device(): jnp.einsum('ijcd,sic->sjd', accumulate_slopes, left_block, preferred_elem...  9.6 us
    unnamed x46, local copies, waits for them, and re-layouts  7.3 us
    split x2, local copies, waits for them, and re-layouts, in_one_piece(): jnp.split(whole, [sum(widths[:k]) for k in range(1, len(widths))], axis=a...  5.78 us
  transfers between devices with their start and end apart: 2, of which 2 were waited for; matrix products, arithmetic and copies ran while one was open for 15% of the time, Pallas kernels for 0%

commit v1 on v0

--- a/solution.py
+++ b/solution.py
@@ -101,7 +101,10 @@
             "ijcd,sic->sjd", accumulate_slopes, left_block, preferred_element_type=jnp.float32
         )
     second_operand_gradient, stored, right_whole = (second_operand_gradient, stored, right_whole)
-    received = lax.all_to_all(stored, "col", split_axis=0, concat_axis=1, tiled=True)
+    received = jnp.concatenate(
+        lax.all_to_all(jnp.stack(jnp.split(stored, lax.psum(1, "col"), axis=0)), "col", 0, 0),
+        axis=1,
+    )
     right_all = right_whole.reshape(alignment_row_count, residue_total_count, operand_channel_width)
     col_span = local_residue_start * max(
         max(1, 96 // local_residue_start), lax.axis_size("col") // 8

time: 279 us -> 364 us (1.30)
  local copies, waits for them, and re-layouts: 70.5 us -> 151 us
    unnamed x46 -> x183, local copies, waits for them, and re-layouts: 7.3 us -> 48.3 us
    another operation x0 -> x65, local copies, waits for them, and re-layouts: none -> 40.1 us  [per_device(): jnp.stack(jnp.split(stored, lax.psum(1, 'col'), axis=0))]
  transfers between devices with their start and end apart: 2 -> 2, of which waited for: 2 -> 2; matrix products, arithmetic and copies ran while one was open for 15% -> 12% of each run, Pallas kernels for 0% -> 0%
where the time goes in v1:
time: 364 us; the launch traced here: 360 us
  local copies, waits for them, and re-layouts  151 us (41%)
  waiting for transfers between devices  147 us (40%)
  matrix products  28.8 us (8%)
  between operations  15.2 us (4%)
  starting transfers between devices  14.4 us (4%)
  other arithmetic  3.94 us (1%)
    all_gather x1, waiting for transfers between devices, in_one_piece(): whole = lax.all_gather(both, axis, axis=dim, tiled=True)  143 us
    unnamed x183, local copies, waits for them, and re-layouts  48.3 us
    another operation x65, local copies, waits for them, and re-layouts, per_device(): jnp.stack(jnp.split(stored, lax.psum(1, 'col'), axis=0))  40.1 us
    reshape x6, local copies, waits for them, and re-layouts, outer_slopes(): backward.astype(jnp.bfloat16)  16.2 us
    convert_element_type x3, local copies, waits for them, and re-layouts, per_device(): products.astype(jnp.bfloat16)  14.5 us
    all_to_all x1, starting transfers between devices, per_device(): lax.all_to_all(jnp.stack(jnp.split(stored, lax.psum(1, 'col'), axis=0)),...  14.3 us
    reshape x3, local copies, waits for them, and re-layouts, per_device(): products.astype(jnp.bfloat16)  10.3 us
    dot_general x3, matrix products, per_device(): jnp.einsum('ijcd,sic->sjd', accumulate_slopes, left_block, preferred_elem...  9.6 us
  transfers between devices with their start and end apart: 2, of which 2 were waited for; matrix products, arithmetic and copies ran while one was open for 12% of the time, Pallas kernels for 0%

profile of v1, /device:TPU:38, one launch (start us, length us, event | category | flops | bytes accessed | tf_op | source)
XLA Modules:
  0.0 360.2 jit_solution(6365624477995590271)
XLA Ops:
  12.9 1.8 convert_multiply_fusion
  14.7 143.4 %all-gather.2.cloned.1.call-done = bf16[192,8192]{1,0:T(8,128)(2,1)} async-done(((bf16[192,128]{1,0:T(8,128)(2,1)}), bf16[192,8192]{1,0:T(8,128)(2,1)}) %all-gather.2.cloned.1.call-update) | async-done | bytes 3145744 | tf_op jit(solution)/shard_map/all_gather | solution.py:10
  158.1 2.2 fusion.42
  163.8 5.8 %copy.27 = bf16[96,4,32,32]{3,2,1,0:T(8,128)(2,1)S(1)} copy(bf16[96,4,32,32]{0,3,2,1:T(8,128)(2,1)} %fusion.4) | data formatting | bytes 1572864 | tf_op jit(solution)/shard_map/convert_element_type | solution.py:84
  169.7 4.1 %reshape.227 = bf16[384,1024]{1,0:T(8,128)(2,1)} reshape(bf16[96,4,32,32]{3,2,1,0:T(8,128)(2,1)S(1)} %copy.27) | data formatting | bytes 1572864 | tf_op jit(solution)/shard_map/reshape | solution.py:84
  181.2 5.4 %copy.31 = bf16[96,4,32,32]{3,2,1,0:T(8,128)(2,1)S(1)} copy(bf16[96,4,32,32]{0,3,2,1:T(8,128)(2,1)} %fusion.5) | data formatting | bytes 1572864 | tf_op jit(solution)/shard_map/convert_element_type | solution.py:84
  186.6 4.0 %reshape.229 = bf16[384,1024]{1,0:T(8,128)(2,1)} reshape(bf16[96,4,32,32]{3,2,1,0:T(8,128)(2,1)S(1)} %copy.31) | data formatting | bytes 1572864 | tf_op jit(solution)/shard_map/reshape | solution.py:84
  190.6 1.6 fusion.14
  235.6 3.2 copy.35
  239.2 2.2 reshape.231
  282.9 14.3 %all-to-all-start = ((bf16[64,4,512]{2,1,0:T(4,128)(2,1)}), bf16[64,4,512]{2,1,0:T(4,128)(2,1)}, u32[]{:S(2)}, u32[]{:S(2)}) async-start(bf16[64,4,512]{2,1,0:T(4,128)(2,1)} %constant_dynamic-update-slice_fusion), calls=%async_computation | async-start | bytes 524288 | tf_op jit(solution)/shard_map/all_to_all | solution.py:105
  297.3 2.7 split.261
  300.0 3.1 copy.21
  305.1 2.9 copy.72
  308.0 1.8 copy.71
  311.2 3.8 %reshape.240 = bf16[96,4,32,32]{3,2,1,0:T(8,128)(2,1)S(1)} reshape(bf16[384,1024]{1,0:T(8,128)(2,1)} %multiply_convert_fusion.4) | data formatting | bytes 1572864 | tf_op jit(solution)/shard_map/reshape | solution.py:49
  316.2 4.9 %reshape.241 = bf16[96,4,32,32]{3,2,1,0:T(8,128)(2,1)} reshape(bf16[384,1024]{1,0:T(8,128)(2,1)} %multiply_convert_fusion.3) | data formatting | bytes 1572864 | tf_op jit(solution)/shard_map/reshape | solution.py:49
  322.2 3.9 %reshape.242 = bf16[64,4,32,32]{3,2,1,0:T(8,128)(2,1)} reshape(bf16[256,1024]{1,0:T(8,128)(2,1)} %fusion.8) | data formatting | bytes 1048576 | tf_op jit(solution)/shard_map/reshape | solution.py:49
  326.2 4.7 %fusion.20 = f32[96,4,32]{0,2,1:T(8,128)S(1)} fusion(bf16[96,4,32,32]{3,2,1,0:T(8,128)(2,1)S(1)} %reshape.240, bf16[96,96,32]{1,0,2:T(8,128)(2,1)} %copy-done.3), kind=kOutput, calls=%fused_computation.34 | convolution fusion | flops 75497472 | bytes 1425408 | tf_op jit(solution)/shard_map/ijcd,sic->sjd/dot_general | solution.py:100
  330.9 3.5 fusion.27
  335.9 3.2 all-to-all-done
  343.3 1.6 reshape.235
  347.0 2.1 convolution_bitcast_fusion.1
  349.9 2.0 fusion.50
  (299 shorter events, 116.7 us)
Async XLA Ops:
  7.2 166.6 %copy-start = (bf16[1024,128]{1,0:T(8,128)(2,1)S(1)}, bf16[1024,128]{1,0:T(8,128)(2,1)}, u32[]{:S(2)}) copy-start(bf16[1024,128]{1,0:T(8,128)(2,1)} %param.9) | copy-start | bytes 786436
  7.2 150.9 %all-gather.2.cloned.1.call-start = ((), (), s32[]{:S(2)}) async-start(), calls=%async_computation.1 | async-start | bytes 3194880 | tf_op jit(solution)/shard_map/all_gather | solution.py:10
  239.0 20.1 %copy-start.38 = (bf16[1,4,512]{2,1,0:T(4,128)(2,1)S(1)}, bf16[1,4,512]{2,1,0:T(4,128)(2,1)}, u32[]{:S(2)}) copy-start(bf16[1,4,512]{2,1,0:T(4,128)(2,1)} %stack.219) | copy-start | bytes 12292
  239.1 20.7 %copy-start.37 = (bf16[1,4,512]{2,1,0:T(4,128)(2,1)S(1)}, bf16[1,4,512]{2,1,0:T(4,128)(2,1)}, u32[]{:S(2)}) copy-start(bf16[1,4,512]{2,1,0:T(4,128)(2,1)} %stack.220) | copy-start | bytes 12292
  239.1 21.2 %copy-start.36 = (bf16[1,4,512]{2,1,0:T(4,128)(2,1)S(1)}, bf16[1,4,512]{2,1,0:T(4,128)(2,1)}, u32[]{:S(2)}) copy-start(bf16[1,4,512]{2,1,0:T(4,128)(2,1)} %stack.221) | copy-start | bytes 12292
  239.1 21.8 %copy-start.34 = (bf16[1,4,512]{2,1,0:T(4,128)(2,1)S(1)}, bf16[1,4,512]{2,1,0:T(4,128)(2,1)}, u32[]{:S(2)}) copy-start(bf16[1,4,512]{2,1,0:T(4,128)(2,1)} %stack.222) | copy-start | bytes 12292
  239.1 22.4 %copy-start.35 = (bf16[1,4,512]{2,1,0:T(4,128)(2,1)S(1)}, bf16[1,4,512]{2,1,0:T(4,128)(2,1)}, u32[]{:S(2)}) copy-start(bf16[1,4,512]{2,1,0:T(4,128)(2,1)} %stack.223) | copy-start | bytes 12292
  239.1 23.0 %copy-start.33 = (bf16[1,4,512]{2,1,0:T(4,128)(2,1)S(1)}, bf16[1,4,512]{2,1,0:T(4,128)(2,1)}, u32[]{:S(2)}) copy-start(bf16[1,4,512]{2,1,0:T(4,128)(2,1)} %stack.224) | copy-start | bytes 12292
  239.1 23.6 %copy-start.32 = (bf16[1,4,512]{2,1,0:T(4,128)(2,1)S(1)}, bf16[1,4,512]{2,1,0:T(4,128)(2,1)}, u32[]{:S(2)}) copy-start(bf16[1,4,512]{2,1,0:T(4,128)(2,1)} %stack.225) | copy-start | bytes 12292
  239.1 24.2 %copy-start.31 = (bf16[1,4,512]{2,1,0:T(4,128)(2,1)S(1)}, bf16[1,4,512]{2,1,0:T(4,128)(2,1)}, u32[]{:S(2)}) copy-start(bf16[1,4,512]{2,1,0:T(4,128)(2,1)} %stack.226) | copy-start | bytes 12292
  239.1 24.8 %copy-start.30 = (bf16[1,4,512]{2,1,0:T(4,128)(2,1)S(1)}, bf16[1,4,512]{2,1,0:T(4,128)(2,1)}, u32[]{:S(2)}) copy-start(bf16[1,4,512]{2,1,0:T(4,128)(2,1)} %stack.227) | copy-start | bytes 12292
  239.1 25.3 %copy-start.29 = (bf16[1,4,512]{2,1,0:T(4,128)(2,1)S(1)}, bf16[1,4,512]{2,1,0:T(4,128)(2,1)}, u32[]{:S(2)}) copy-start(bf16[1,4,512]{2,1,0:T(4,128)(2,1)} %stack.228) | copy-start | bytes 12292
  239.1 25.9 %copy-start.28 = (bf16[1,4,512]{2,1,0:T(4,128)(2,1)S(1)}, bf16[1,4,512]{2,1,0:T(4,128)(2,1)}, u32[]{:S(2)}) copy-start(bf16[1,4,512]{2,1,0:T(4,128)(2,1)} %stack.229) | copy-start | bytes 12292
  239.2 26.5 %copy-start.27 = (bf16[1,4,512]{2,1,0:T(4,128)(2,1)S(1)}, bf16[1,4,512]{2,1,0:T(4,128)(2,1)}, u32[]{:S(2)}) copy-start(bf16[1,4,512]{2,1,0:T(4,128)(2,1)} %stack.230) | copy-start | bytes 12292
  239.2 27.1 %copy-start.26 = (bf16[1,4,512]{2,1,0:T(4,128)(2,1)S(1)}, bf16[1,4,512]{2,1,0:T(4,128)(2,1)}, u32[]{:S(2)}) copy-start(bf16[1,4,512]{2,1,0:T(4,128)(2,1)} %stack.231) | copy-start | bytes 12292
  239.2 27.7 %copy-start.25 = (bf16[1,4,512]{2,1,0:T(4,128)(2,1)S(1)}, bf16[1,4,512]{2,1,0:T(4,128)(2,1)}, u32[]{:S(2)}) copy-start(bf16[1,4,512]{2,1,0:T(4,128)(2,1)} %stack.232) | copy-start | bytes 12292
  239.2 28.3 %copy-start.24 = (bf16[1,4,512]{2,1,0:T(4,128)(2,1)S(1)}, bf16[1,4,512]{2,1,0:T(4,128)(2,1)}, u32[]{:S(2)}) copy-start(bf16[1,4,512]{2,1,0:T(4,128)(2,1)} %stack.233) | copy-start | bytes 12292
  239.2 28.9 %copy-start.23 = (bf16[1,4,512]{2,1,0:T(4,128)(2,1)S(1)}, bf16[1,4,512]{2,1,0:T(4,128)(2,1)}, u32[]{:S(2)}) copy-start(bf16[1,4,512]{2,1,0:T(4,128)(2,1)} %stack.234) | copy-start | bytes 12292
  239.2 29.5 %copy-start.22 = (bf16[1,4,512]{2,1,0:T(4,128)(2,1)S(1)}, bf16[1,4,512]{2,1,0:T(4,128)(2,1)}, u32[]{:S(2)}) copy-start(bf16[1,4,512]{2,1,0:T(4,128)(2,1)} %stack.235) | copy-start | bytes 12292
  239.2 30.0 %copy-start.21 = (bf16[1,4,512]{2,1,0:T(4,128)(2,1)S(1)}, bf16[1,4,512]{2,1,0:T(4,128)(2,1)}, u32[]{:S(2)}) copy-start(bf16[1,4,512]{2,1,0:T(4,128)(2,1)} %stack.236) | copy-start | bytes 12292
  239.2 30.6 %copy-start.20 = (bf16[1,4,512]{2,1,0:T(4,128)(2,1)S(1)}, bf16[1,4,512]{2,1,0:T(4,128)(2,1)}, u32[]{:S(2)}) copy-start(bf16[1,4,512]{2,1,0:T(4,128)(2,1)} %stack.237) | copy-start | bytes 12292
  239.2 31.2 %copy-start.19 = (bf16[1,4,512]{2,1,0:T(4,128)(2,1)S(1)}, bf16[1,4,512]{2,1,0:T(4,128)(2,1)}, u32[]{:S(2)}) copy-start(bf16[1,4,512]{2,1,0:T(4,128)(2,1)} %stack.238) | copy-start | bytes 12292
  242.4 57.5 %copy-start.13 = (bf16[256,128]{1,0:T(8,128)(2,1)}, bf16[256,128]{1,0:T(8,128)(2,1)S(1)}, u32[]{:S(2)}) copy-start(bf16[256,128]{1,0:T(8,128)(2,1)S(1)} %fusion.18) | copy-start | bytes 196612
  282.9 56.2 %all-to-all-start = ((bf16[64,4,512]{2,1,0:T(4,128)(2,1)}), bf16[64,4,512]{2,1,0:T(4,128)(2,1)}, u32[]{:S(2)}, u32[]{:S(2)}) async-start(bf16[64,4,512]{2,1,0:T(4,128)(2,1)} %constant_dynamic-update-slice_fusion), calls=%async_computation | async-start | bytes 524288 | tf_op jit(solution)/shard_map/all_to_all | solution.py:105
  (37 other events, 321.0 us)
Sparse Core Ops, SparseCore 0:
  11.4 146.6 all-gather.1
